TPU v7x, 32 devices: a whole 2x2x4 slice. The times are simulated.
32 devices in a mesh: dp: 16 (over z, y, core), cp: 2 (over x).
Axes of the slice: x: 2, y: 2, z: 4, core: 2. Of those that a mesh axis runs over, the one named last changes fastest.
Arguments:
- x_source: bfloat16 [16, 1024, 768], P(None, ('cp', 'dp')), may hold values from -6 to 6
- cotangent: bfloat16 [16, 1024, 768], P('dp', 'cp'), may hold values from -6 to 6
- lengths: int32 [16], replicated, may hold values from 1 to 1024, 10240 in all
- dealing: int32 [16], replicated, may hold values from 0 to 15, each once
- qkv_weight: float32 [768, 2304], P('cp', 'dp'), may hold values from -0.21875 to 0.21875
- proj_weight: float32 [768, 768], P('cp', 'dp'), may hold values from -2 to 2
- up_weight: float32 [768, 3072], P('cp', 'dp'), may hold values from -0.21875 to 0.21875
- down_weight: float32 [3072, 768], P('cp', 'dp'), may hold values from -0.109375 to 0.109375
- first_gain: float32 [768], P('dp'), may hold values from 0.1 to 1.9
- first_shift: float32 [768], P('dp'), may hold values from -1.75 to 1.75
- proj_bias: float32 [768], P('dp'), may hold values from -1.75 to 1.75
- second_gain: float32 [768], P('dp'), may hold values from 0.1 to 1.9
- second_shift: float32 [768], P('dp'), may hold values from -1.75 to 1.75
- up_bias: float32 [3072], P('dp'), may hold values from -3 to 3
- down_bias: float32 [768], P('dp'), may hold values from -1.75 to 1.75
Outputs:
- output: bfloat16 [16, 1024, 768], P('dp', 'cp')
- input_grad: bfloat16 [16, 1024, 768], P(None, ('cp', 'dp'))
- qkv_grad: float32 [768, 2304], P('cp', 'dp')
- proj_grad: float32 [768, 768], P('cp', 'dp')
- up_grad: float32 [768, 3072], P('cp', 'dp')
- down_grad: float32 [3072, 768], P('cp', 'dp')
- first_gain_grad: float32 [768], P('dp')
- first_shift_grad: float32 [768], P('dp')
- proj_bias_grad: float32 [768], P('dp')
- second_gain_grad: float32 [768], P('dp')
- second_shift_grad: float32 [768], P('dp')
- up_bias_grad: float32 [3072], P('dp')
- down_bias_grad: float32 [768], P('dp')
Inputs may be any that keep to these rules, and one draw needn't show every extreme that they name: The lengths sum to 10240 and the longest is exactly 1024. `dealing`: a permutation of the sequence numbers.
All inputs are finite; a program needn't handle non-finite values.
Results may differ from a plain program's by a relative error of at most 0.019.
Values may be sent and summed in bfloat16 or wider, within the bound.
A program may use at most 192 MiB of HBM per device.

v0:
```python
import math

import jax
import jax.numpy as jnp
from jax import lax
from jax.sharding import PartitionSpec as P

HEADS = 12
HEAD_DIM = 64


EPSILON = 1e-05
NEG_BIG = -1e30
TANH_SCALE = 0.7978845608028654
CUBIC_TERM = 0.044715


def layer_norm(values, scaling, offset):
    centered = values - jnp.mean(values, axis=-1, keepdims=True)
    spread = jnp.mean(centered * centered, axis=-1, keepdims=True)
    return centered * lax.rsqrt(spread + EPSILON) * scaling + offset


def gelu_tanh(values):
    return (
        0.5
        * values
        * (1.0 + jnp.tanh(TANH_SCALE * (values + CUBIC_TERM * values * values * values)))
    )


def grouped(array, block_seqs):
    return array.reshape(
        (array.shape[0] // block_seqs, block_seqs, array.shape[1], HEADS, array.shape[2] // HEADS)
    )


def grouped_stats(array, block_seqs):
    return array.reshape((array.shape[0] // block_seqs, block_seqs) + array.shape[1:])


def joined(array):
    return array.reshape(
        (array.shape[0] * array.shape[1], array.shape[2], array.shape[3] * array.shape[4])
    )


def masked_scores(queries, key_rows, query_start, score_scale):
    scores = (
        jnp.einsum("bqhd,bkhd->bhqk", queries, key_rows, preferred_element_type=jnp.float32)
        * score_scale
    )
    query_pos = query_start + jnp.arange(queries.shape[1])
    key_pos = jnp.arange(key_rows.shape[1])
    return jnp.where(key_pos[None, :] <= query_pos[:, None], scores, NEG_BIG)


def attend(inputs, query_start, score_scale):
    queries, key_rows, val_rows = inputs
    scores = masked_scores(queries, key_rows, query_start, score_scale)
    row_top = jnp.max(scores, axis=-1, keepdims=True)
    exponent = jnp.exp(scores - row_top)
    totals = jnp.sum(exponent, axis=-1, keepdims=True)
    weights = (exponent / totals).astype(jnp.bfloat16)
    attended = jnp.einsum("bhqk,bkhd->bqhd", weights, val_rows, preferred_element_type=jnp.float32)
    return (attended.astype(jnp.bfloat16), (row_top + jnp.log(totals))[..., 0])


def rows_back(inputs, query_start, score_scale):
    queries, key_rows, val_rows, grad_rows, log_total = inputs
    scores = masked_scores(queries, key_rows, query_start, score_scale)
    weights = jnp.exp(scores - log_total[..., None])
    grad_weights = jnp.einsum(
        "bqhd,bkhd->bhqk", grad_rows, val_rows, preferred_element_type=jnp.float32
    )
    delta_rows = jnp.sum(weights * grad_weights, axis=-1)
    grad_scores = (weights * (grad_weights - delta_rows[..., None])).astype(jnp.bfloat16)
    grad_query = (
        jnp.einsum("bhqk,bkhd->bqhd", grad_scores, key_rows, preferred_element_type=jnp.float32)
        * score_scale
    )
    grad_keys = (
        jnp.einsum("bhqk,bqhd->bkhd", grad_scores, queries, preferred_element_type=jnp.float32)
        * score_scale
    )
    grad_vals = jnp.einsum(
        "bhqk,bqhd->bkhd",
        weights.astype(jnp.bfloat16),
        grad_rows,
        preferred_element_type=jnp.float32,
    )
    return (grad_query, grad_keys, grad_vals)


def fetch_weights(
    qkv_weight,
    proj_weight,
    up_weight,
    down_weight,
    first_gain,
    first_shift,
    proj_bias,
    second_gain,
    second_shift,
    up_bias,
    down_bias,
):
    qkv_part, proj_part, up_part, down_part = (
        lax.all_gather(qkv_weight.astype(jnp.bfloat16), "cp", axis=0, tiled=True),
        lax.all_gather(proj_weight.astype(jnp.bfloat16), "cp", axis=0, tiled=True),
        lax.all_gather(up_weight.astype(jnp.bfloat16), "cp", axis=0, tiled=True),
        lax.all_gather(down_weight.astype(jnp.bfloat16), "cp", axis=0, tiled=True),
    )
    return (
        lax.all_gather(qkv_part, "dp", axis=1, tiled=True),
        lax.all_gather(proj_part, "dp", axis=1, tiled=True),
        lax.all_gather(up_part, "dp", axis=1, tiled=True),
        lax.all_gather(down_part, "dp", axis=1, tiled=True),
        lax.all_gather(first_gain.astype(jnp.bfloat16), "dp", axis=0, tiled=True),
        lax.all_gather(first_shift.astype(jnp.bfloat16), "dp", axis=0, tiled=True),
        lax.all_gather(proj_bias.astype(jnp.bfloat16), "dp", axis=0, tiled=True),
        lax.all_gather(second_gain.astype(jnp.bfloat16), "dp", axis=0, tiled=True),
        lax.all_gather(second_shift.astype(jnp.bfloat16), "dp", axis=0, tiled=True),
        lax.all_gather(up_bias.astype(jnp.bfloat16), "dp", axis=0, tiled=True),
        lax.all_gather(down_bias.astype(jnp.bfloat16), "dp", axis=0, tiled=True),
    )


def mat_rows(left, right):
    return jnp.einsum("sqd,de->sqe", left, right, preferred_element_type=jnp.float32)


def mat_back(left, right):
    return jnp.einsum("sqe,de->sqd", left, right, preferred_element_type=jnp.float32)


def mat_grad(left, right):
    return jnp.einsum("sqd,sqe->de", left, right, preferred_element_type=jnp.float32)


def local(
    x_source,
    cotangent,
    lengths,
    dealing,
    qkv_weight,
    proj_weight,
    up_weight,
    down_weight,
    first_gain,
    first_shift,
    proj_bias,
    second_gain,
    second_shift,
    up_bias,
    down_bias,
):
    groups = lax.axis_size("dp")
    seqs_all, piece_rows, features = x_source.shape
    seq_group = seqs_all // groups
    span_rows = groups * piece_rows
    score_scale = HEAD_DIM ** (-0.5)
    block_seqs = math.gcd(seq_group, max(1, 512 // span_rows))
    owners = jnp.argsort(dealing)
    send_order = owners.reshape(groups, seq_group).T.reshape(-1)
    outgoing = x_source[send_order].reshape(seq_group, span_rows, features)
    arrived = lax.all_to_all(outgoing, "dp", split_axis=1, concat_axis=1, tiled=True)
    first_slot = lax.axis_index("dp") * seq_group
    my_lengths = lax.dynamic_slice_in_dim(lengths[owners], first_slot, seq_group)
    query_start = lax.axis_index("cp") * span_rows
    positions = query_start + jnp.arange(span_rows)
    live_rows = positions[None, :] < my_lengths[:, None]
    fetched = fetch_weights(
        qkv_weight,
        proj_weight,
        up_weight,
        down_weight,
        first_gain,
        first_shift,
        proj_bias,
        second_gain,
        second_shift,
        up_bias,
        down_bias,
    )
    qkv_full, proj_full, up_full, down_full = (fetched[0], fetched[1], fetched[2], fetched[3])
    gain_one, shift_one, bias_proj, gain_two, shift_two, bias_up, bias_down = [
        vector.astype(jnp.float32) for vector in fetched[4:]
    ]
    inputs_f = arrived.astype(jnp.float32)
    norm_one, back_one = jax.vjp(layer_norm, inputs_f, gain_one, shift_one)
    act_one = norm_one.astype(jnp.bfloat16)
    mixed_rows = mat_rows(act_one, qkv_full).astype(jnp.bfloat16)
    queries = mixed_rows[..., :features]
    kv_local = mixed_rows[..., features:]
    kv_all = lax.all_gather(kv_local, "cp", axis=1, tiled=True)
    attended, log_total = lax.map(
        lambda inputs: attend(inputs, query_start, score_scale),
        (
            grouped(queries, block_seqs),
            grouped(kv_all[..., :features], block_seqs),
            grouped(kv_all[..., features:], block_seqs),
        ),
    )
    attended = joined(attended)
    log_total = log_total.reshape((seq_group,) + log_total.shape[2:])
    residual = inputs_f + mat_rows(attended, proj_full) + bias_proj
    norm_two, back_two = jax.vjp(layer_norm, residual, gain_two, shift_two)
    act_two = norm_two.astype(jnp.bfloat16)
    up_raw = mat_rows(act_two, up_full) + bias_up
    hidden, back_gelu = jax.vjp(gelu_tanh, up_raw)
    hid_low = hidden.astype(jnp.bfloat16)
    result = residual + mat_rows(hid_low, down_full) + bias_down
    output = jnp.where(live_rows[..., None], result, 0.0).astype(jnp.bfloat16)
    fetched = fetch_weights(
        qkv_weight,
        proj_weight,
        up_weight,
        down_weight,
        first_gain,
        first_shift,
        proj_bias,
        second_gain,
        second_shift,
        up_bias,
        down_bias,
    )
    qkv_full, proj_full, up_full, down_full = (fetched[0], fetched[1], fetched[2], fetched[3])
    gain_one, gain_two = (fetched[4].astype(jnp.float32), fetched[7].astype(jnp.float32))
    grad_out = jnp.where(live_rows[..., None], cotangent.astype(jnp.float32), 0.0)
    grad_low = grad_out.astype(jnp.bfloat16)
    grad_down = mat_grad(hid_low, grad_low)
    grad_bias_down = jnp.sum(grad_out, axis=(0, 1))
    grad_hidden = mat_back(grad_low, down_full)
    grad_up_raw = back_gelu(grad_hidden)[0].astype(jnp.bfloat16)
    grad_up = mat_grad(act_two, grad_up_raw)
    grad_bias_up = jnp.sum(grad_up_raw.astype(jnp.float32), axis=(0, 1))
    grad_act_two = mat_back(grad_up_raw, up_full)
    grad_resid, grad_gain_two, grad_shift_two = back_two(grad_act_two)
    grad_resid = grad_resid + grad_out
    grad_bias_proj = jnp.sum(grad_resid, axis=(0, 1))
    resid_low = grad_resid.astype(jnp.bfloat16)
    grad_proj = mat_grad(attended, resid_low)
    grad_attended = mat_back(resid_low, proj_full).astype(jnp.bfloat16)
    kv_back = lax.all_gather(kv_local, "cp", axis=1, tiled=True)
    key_rows = kv_back[..., :features]
    val_rows = kv_back[..., features:]
    grad_query, grad_keys, grad_vals = lax.map(
        lambda inputs: rows_back(inputs, query_start, score_scale),
        (
            grouped(queries, block_seqs),
            grouped(key_rows, block_seqs),
            grouped(val_rows, block_seqs),
            grouped(grad_attended, block_seqs),
            grouped_stats(log_total, block_seqs),
        ),
    )
    grad_keys, grad_vals = (
        lax.psum_scatter(
            joined(grad_keys).astype(jnp.bfloat16), "cp", scatter_dimension=1, tiled=True
        ).astype(jnp.float32),
        lax.psum_scatter(
            joined(grad_vals).astype(jnp.bfloat16), "cp", scatter_dimension=1, tiled=True
        ).astype(jnp.float32),
    )
    grad_mixed = jnp.concatenate([joined(grad_query), grad_keys, grad_vals], axis=-1).astype(
        jnp.bfloat16
    )
    grad_qkv = mat_grad(act_one, grad_mixed)
    grad_act_one = mat_back(grad_mixed, qkv_full)
    grad_input, grad_gain_one, grad_shift_one = back_one(grad_act_one)
    grad_input = (grad_input + grad_resid).astype(jnp.bfloat16)
    returned = lax.all_to_all(grad_input, "dp", split_axis=1, concat_axis=0, tiled=True)
    input_grad = returned[dealing]
    (
        grad_qkv,
        grad_proj,
        grad_up,
        grad_down,
        grad_gain_one,
        grad_shift_one,
        grad_bias_proj,
        grad_gain_two,
        grad_shift_two,
        grad_bias_up,
        grad_bias_down,
    ) = (
        lax.psum_scatter(
            grad_qkv.astype(jnp.bfloat16), "dp", scatter_dimension=1, tiled=True
        ).astype(jnp.float32),
        lax.psum_scatter(
            grad_proj.astype(jnp.bfloat16), "dp", scatter_dimension=1, tiled=True
        ).astype(jnp.float32),
        lax.psum_scatter(
            grad_up.astype(jnp.bfloat16), "dp", scatter_dimension=1, tiled=True
        ).astype(jnp.float32),
        lax.psum_scatter(
            grad_down.astype(jnp.bfloat16), "dp", scatter_dimension=1, tiled=True
        ).astype(jnp.float32),
        lax.psum_scatter(
            grad_gain_one.astype(jnp.bfloat16), "dp", scatter_dimension=0, tiled=True
        ).astype(jnp.float32),
        lax.psum_scatter(
            grad_shift_one.astype(jnp.bfloat16), "dp", scatter_dimension=0, tiled=True
        ).astype(jnp.float32),
        lax.psum_scatter(
            grad_bias_proj.astype(jnp.bfloat16), "dp", scatter_dimension=0, tiled=True
        ).astype(jnp.float32),
        lax.psum_scatter(
            grad_gain_two.astype(jnp.bfloat16), "dp", scatter_dimension=0, tiled=True
        ).astype(jnp.float32),
        lax.psum_scatter(
            grad_shift_two.astype(jnp.bfloat16), "dp", scatter_dimension=0, tiled=True
        ).astype(jnp.float32),
        lax.psum_scatter(
            grad_bias_up.astype(jnp.bfloat16), "dp", scatter_dimension=0, tiled=True
        ).astype(jnp.float32),
        lax.psum_scatter(
            grad_bias_down.astype(jnp.bfloat16), "dp", scatter_dimension=0, tiled=True
        ).astype(jnp.float32),
    )
    grad_qkv, grad_proj, grad_up, grad_down = (
        lax.psum_scatter(
            grad_qkv.astype(jnp.bfloat16), "cp", scatter_dimension=0, tiled=True
        ).astype(jnp.float32),
        lax.psum_scatter(
            grad_proj.astype(jnp.bfloat16), "cp", scatter_dimension=0, tiled=True
        ).astype(jnp.float32),
        lax.psum_scatter(
            grad_up.astype(jnp.bfloat16), "cp", scatter_dimension=0, tiled=True
        ).astype(jnp.float32),
        lax.psum_scatter(
            grad_down.astype(jnp.bfloat16), "cp", scatter_dimension=0, tiled=True
        ).astype(jnp.float32),
    )
    (
        grad_gain_one,
        grad_shift_one,
        grad_bias_proj,
        grad_gain_two,
        grad_shift_two,
        grad_bias_up,
        grad_bias_down,
    ) = lax.psum(
        (
            grad_gain_one,
            grad_shift_one,
            grad_bias_proj,
            grad_gain_two,
            grad_shift_two,
            grad_bias_up,
            grad_bias_down,
        ),
        "cp",
    )
    return (
        output,
        input_grad,
        grad_qkv,
        grad_proj,
        grad_up,
        grad_down,
        grad_gain_one,
        grad_shift_one,
        grad_bias_proj,
        grad_gain_two,
        grad_shift_two,
        grad_bias_up,
        grad_bias_down,
    )


def solution(mesh):
    in_specs = (
        P(None, ("cp", "dp"), None),
        P("dp", "cp", None),
        P(),
        P(),
        P("cp", "dp"),
        P("cp", "dp"),
        P("cp", "dp"),
        P("cp", "dp"),
        P("dp"),
        P("dp"),
        P("dp"),
        P("dp"),
        P("dp"),
        P("dp"),
        P("dp"),
    )
    out_specs = (
        P("dp", "cp", None),
        P(None, ("cp", "dp"), None),
        P("cp", "dp"),
        P("cp", "dp"),
        P("cp", "dp"),
        P("cp", "dp"),
        P("dp"),
        P("dp"),
        P("dp"),
        P("dp"),
        P("dp"),
        P("dp"),
        P("dp"),
    )
    return jax.shard_map(local, mesh=mesh, in_specs=in_specs, out_specs=out_specs, check_vma=False)
```

profile of v0, /device:TPU:0, one launch (start us, length us, event | category | flops | bytes accessed | tf_op | source)
XLA Modules:
  0.0 742.9 jit_solution(12308336290372131124)
XLA Ops:
  8.3 6.8 all_gather.59
  19.4 5.5 reduce.22
  25.9 6.2 all-to-all-start
  35.5 69.5 %all-reduce.16 = (bf16[768]{0:T(1024)(128)(2,1)S(1)}, bf16[768]{0:T(1024)(128)(2,1)S(1)}, bf16[768]{0:T(1024)(128)(2,1)S(1)}, bf16[768]{0:T(1024)(128)(2,1)S(1)}...) all-reduce(bf16[768]{0:T(1024)(128)(2,1)S(1)} %dynamic-update-slice, ...), channel_id=1, replica_groups=mesh['dp'=16,'cp'=2] {'dp'}, use_global_device_ids=true, to_apply=%add.1 | all-reduce | flops 6912 | bytes 27648
  106.5 4.2 fusion.13
  113.6 5.1 all_gather.62
  118.8 10.2 %all_gather.67 = bf16[768,192]{0,1:T(8,128)(2,1)} all-gather(bf16[384,192]{0,1:T(8,128)(2,1)S(1)} %convert_element_type.266), channel_id=1, replica_groups=mesh['dp'=16,'cp'=2] {'cp'}, dimensions={0}, use_global_device_ids=true | all-gather | bytes 442368 | tf_op jit(solution)/shard_map/all_gather | solution.py:111
  129.2 9.2 %all_gather.70 = bf16[3072,48]{0,1:T(8,128)(2,1)} all-gather(bf16[1536,48]{0,1:T(8,128)(2,1)S(1)} %convert_element_type.270), channel_id=1, replica_groups=mesh['dp'=16,'cp'=2] {'cp'}, dimensions={0}, use_global_device_ids=true | all-gather | bytes 442368 | tf_op jit(solution)/shard_map/all_gather | solution.py:112
  142.0 19.6 %all-gather.8.cloned.1.call-done = bf16[1,1024,1536]{2,1,0:T(8,128)(2,1)} async-done(((bf16[1,512,1536]{2,1,0:T(8,128)(2,1)}), bf16[1,1024,1536]{2,1,0:T(8,128)(2,1)}) %all-gather.8.cloned.1.call-update) | async-done | bytes 3145744 | tf_op jit(solution)/shard_map/all_gather | solution.py:196
  161.6 3.7 fusion.68
  167.0 3.2 copy.48
  170.2 12.1 %fusion.6 = (f32[12,512]{1,0:T(8,128)S(1)}, f32[12,512,1024]{2,1,0:T(8,128)}) fusion(pred[512,1024]{1,0:T(8,128)(4,1)S(1)} %iota_compare_fusion, bf16[512,12,64]{0,2,1:T(8,128)(2,1)} %bitcast.121, bf16[1024,12,64]{0,2,1:T(8,128)(2,1)S(1)} %bitcast.119), kind=kOutput, calls=%fused_computation.18 | convolution fusion | flops 824174592 | bytes 28073984 | tf_op jit(solution)/shard_map/while/body/eval_jaxpr/bqhd,bkhd->bhqk/dot_general | solution.py:50
  182.3 12.5 %fusion = f32[12,512]{1,0:T(8,128)S(1)} fusion(f32[12,512]{1,0:T(8,128)S(1)} %get-tuple-element.102, f32[12,512,1024]{2,1,0:T(8,128)} %get-tuple-element.103, pred[512,1024]{1,0:T(8,128)(4,1)S(1)} %iota_compare_fusion), kind=kLoop, calls=%fused_computation.9 | loop fusion | flops 25159680 | bytes 25739264 | tf_op jit(solution)/shard_map/while/body/eval_jaxpr/reduce_sum | solution.py:63
  194.8 3.2 copy-done.3
  198.0 8.5 %fusion.36 = bf16[12,64,512]{2,1,0:T(8,128)(2,1)} fusion(bf16[1024,12,64]{0,2,1:T(8,128)(2,1)S(1)} %bitcast.124, f32[12,512]{1,0:T(8,128)S(1)} %fusion, f32[12,512]{1,0:T(8,128)S(1)} %get-tuple-element.102, f32[12,512,1024]{2,1,0:T(8,128)S(1)} %copy-done.3, pred[512,1024]{1,0:T(8,128)(4,1)S(1)} %iota_compare_fusion), kind=kOutput, calls=%fused_computation.70 | convolution fusion | flops 837156864 | bytes 28098560 | tf_op jit(solution)/shard_map/while/body/eval_jaxpr/bhqk,bkhd->bqhd/dot_general | solution.py:65
  206.5 2.4 fusion.70
  209.2 45.8 %all-gather.12.cloned.1.call-done = bf16[768,3072]{0,1:T(8,128)(2,1)} async-done(((bf16[768,192]{0,1:T(8,128)(2,1)}), bf16[768,3072]{0,1:T(8,128)(2,1)}) %all-gather.12.cloned.1.call-update) | async-done | bytes 4718608 | tf_op jit(solution)/shard_map/all_gather | solution.py:117
  255.0 7.0 fusion.64
  262.0 46.8 %all-gather.14.cloned.1.call-done = bf16[3072,768]{0,1:T(8,128)(2,1)} async-done(((bf16[3072,48]{0,1:T(8,128)(2,1)}), bf16[3072,768]{0,1:T(8,128)(2,1)}) %all-gather.14.cloned.1.call-update) | async-done | bytes 4718608 | tf_op jit(solution)/shard_map/all_gather | solution.py:118
  308.8 11.8 %fusion.71 = (bf16[3072]{0:T(1024)(128)(2,1)S(1)}, bf16[512,3072]{1,0:T(8,128)(2,1)S(1)}) fusion(bf16[3072,768]{0,1:T(8,128)(2,1)} %all-gather.14.cloned.1.call-done, bf16[1,512,768]{2,1,0:T(8,128)(2,1)} %param.16, pred[512]{0:T(512)(128)(4,1)S(1)} %broadcast_compare_fusion, f32[512,3072]{1,0:T(8,128)} %fusion.64, f32[3072]{0:T(1024)S(1)} %convert_element_type.268), kind=kOutput, calls=%fused_computation.119 | convolution fusion | flops 2457990144 | bytes 14961152 | tf_op jit(solution)/shard_map/sqe,de->sqd/dot_general | solution.py:134
  320.7 2.8 fusion.29
  325.9 2.1 convolution_convert_fusion.4
  327.9 3.5 convolution_convert_fusion.5
  331.4 2.4 copy.51
  334.0 17.9 %multiply_reduce_fusion = (f32[12,512]{1,0:T(8,128)S(1)}, f32[12,512,1024]{2,1,0:T(8,128)}) fusion(f32[12,512]{1,0:T(8,128)S(1)} %log_add_fusion, f32[12,512,1024]{2,1,0:T(8,128)} %get-tuple-element.103, pred[512,1024]{1,0:T(8,128)(4,1)S(1)} %iota_compare_fusion, bf16[512,12,64]{0,2,1:T(8,128)(2,1)} %bitcast.132, bf16[1024,12,64]{0,2,1:T(8,128)(2,1)S(1)} %bitcast.125), kind=kOutput, calls=%fused_computation.4 | convolution fusion | flops 836757504 | bytes 53264384 | tf_op jit(solution)/shard_map/while/body/eval_jaxpr/bqhd,bkhd->bhqk/dot_general | solution.py:73
  351.8 13.1 %fusion.20 = bf16[12,64,1024]{2,1,0:T(8,128)(2,1)} fusion(bf16[512,12,64]{0,2,1:T(8,128)(2,1)} %bitcast.133, f32[12,512]{1,0:T(8,128)S(1)} %log_add_fusion, f32[12,512,1024]{2,1,0:T(8,128)} %get-tuple-element.103, pred[512,1024]{1,0:T(8,128)(4,1)S(1)} %iota_compare_fusion), kind=kOutput, calls=%fused_computation.45 | convolution fusion | flops 831258624 | bytes 28073984 | tf_op jit(solution)/shard_map/while/body/eval_jaxpr/bhqk,bqhd->bkhd/dot_general | solution.py:86
  365.0 17.1 %multiply_convert_fusion = bf16[12,512,1024]{2,1,0:T(8,128)(2,1)S(1)} fusion(f32[12,512,1024]{2,1,0:T(8,128)} %get-tuple-element.108, f32[12,512]{1,0:T(8,128)S(1)} %get-tuple-element.107, f32[12,512]{1,0:T(8,128)S(1)} %log_add_fusion, f32[12,512,1024]{2,1,0:T(8,128)} %get-tuple-element.103, pred[512,1024]{1,0:T(8,128)(4,1)S(1)} %iota_compare_fusion), kind=kLoop, calls=%fused_computation.3 | loop fusion | flops 37748736 | bytes 63488000 | tf_op jit(solution)/shard_map/while/body/eval_jaxpr/convert_element_type | solution.py:77
  382.2 4.1 multiply_convert_fusion.2
  387.5 3.3 reduce-scatter.23.cloned.1.call-done
  392.8 6.8 convolution_convert_fusion.2
  400.8 8.1 %convolution_convert_fusion.1 = bf16[3072,768]{0,1:T(8,128)(2,1)} fusion(bf16[1,512,768]{2,1,0:T(8,128)(2,1)S(1)} %copy-done.19, pred[512]{0:T(512)(128)(4,1)S(1)} %broadcast_compare_fusion, f32[512,3072]{1,0:T(8,128)} %fusion.64, f32[3072]{0:T(1024)S(1)} %convert_element_type.268), kind=kOutput, calls=%fused_computation.27 | convolution fusion | flops 2435186688 | bytes 11809280 | tf_op jit(solution)/shard_map/sqd,sqe->de/dot_general | solution.py:138
  410.4 8.5 %multiply_convert_fusion.3 = bf16[12,64,512]{2,1,0:T(8,128)(2,1)S(1)} fusion(bf16[1024,12,64]{0,2,1:T(8,128)(2,1)S(1)} %bitcast.120, bf16[12,512,1024]{2,1,0:T(8,128)(2,1)} %copy-done.4), kind=kOutput, calls=%fused_computation.61 | convolution fusion | flops 806092800 | bytes 14942208 | tf_op jit(solution)/shard_map/while/body/eval_jaxpr/bhqk,bkhd->bqhd/dot_general | solution.py:79
  418.9 27.8 %reduce-scatter.17.cloned.1.call-done = bf16[1,512,768]{1,2,0:T(8,128)(2,1)} async-done(((bf16[1,1024,768]{1,2,0:T(8,128)(2,1)}), bf16[1,512,768]{1,2,0:T(8,128)(2,1)}) %reduce-scatter.17.cloned.1.call-update) | async-done | bytes 786448 | tf_op jit(solution)/shard_map/reduce_scatter | solution.py:259
  446.7 5.4 convolution_convert_fusion
  454.3 6.3 reduce-scatter.33.cloned.1.call-done
  462.2 4.7 fusion.27
  467.9 72.0 %reduce-scatter.25.cloned.1.call-done = bf16[768,192]{0,1:T(8,128)(2,1)} async-done(((bf16[768,3072]{0,1:T(8,128)(2,1)}), bf16[768,192]{0,1:T(8,128)(2,1)}) %reduce-scatter.25.cloned.1.call-update) | async-done | bytes 294928 | tf_op jit(solution)/shard_map/reduce_scatter | solution.py:294
  541.8 2.3 fusion.34
  544.1 59.4 %all-reduce.15 = (bf16[768]{0:T(1024)(128)(2,1)S(1)}, bf16[768]{0:T(1024)(128)(2,1)S(1)}, bf16[768]{0:T(1024)(128)(2,1)S(1)}, bf16[768]{0:T(1024)(128)(2,1)S(1)}...) all-reduce(bf16[768]{0:T(1024)(128)(2,1)S(1)} %dynamic-update-slice, ...), channel_id=1, replica_groups=mesh['dp'=16,'cp'=2] {'dp'}, use_global_device_ids=true, to_apply=%add.6 | all-reduce | flops 8448 | bytes 33792
  604.8 5.4 reduce.23
  611.3 3.6 all-to-all-start.1
  614.9 4.1 reduce-scatter.27.cloned.1.call-done
  619.3 9.1 %fusion.33 = bf16[1,512,768]{2,1,0:T(8,128)(2,1)} fusion(f32[1,512,768]{2,1,0:T(8,128)S(1)} %copy-done.12, bf16[3072,768]{0,1:T(8,128)(2,1)} %all-gather.14.cloned.1.call-done, f32[768]{0:T(1024)S(1)} %convert_element_type.272, pred[512]{0:T(512)(128)(4,1)S(1)} %broadcast_compare_fusion, f32[512,3072]{1,0:T(8,128)} %fusion.64, ...), kind=kOutput, calls=%fused_computation.59 | convolution fusion | flops 2433220608 | bytes 13385216 | tf_op jit(solution)/shard_map/sqd,de->sqe/dot_general | solution.py:130
  628.3 62.2 %reduce-scatter.21.cloned.1.call-done = bf16[768,144]{0,1:T(8,128)(2,1)} async-done(((bf16[768,2304]{0,1:T(8,128)(2,1)}), bf16[768,144]{0,1:T(8,128)(2,1)}) %reduce-scatter.21.cloned.1.call-update) | async-done | bytes 221200 | tf_op jit(solution)/shard_map/reduce_scatter | solution.py:288
  692.8 5.5 all-reduce.14
  700.6 4.3 reduce-scatter.35.cloned.1.call-done
  706.7 12.4 %reduce-scatter.29.cloned.1.call-done = bf16[1536,48]{0,1:T(8,128)(2,1)} async-done(((bf16[3072,48]{0,1:T(8,128)(2,1)}), bf16[1536,48]{0,1:T(8,128)(2,1)}) %reduce-scatter.29.cloned.1.call-update) | async-done | bytes 147472 | tf_op jit(solution)/shard_map/reduce_scatter | solution.py:332
  720.8 13.7 %reduce-scatter.31.cloned.1.call-done = bf16[384,144]{1,0:T(8,128)(2,1)} async-done(((bf16[768,144]{1,0:T(8,128)(2,1)}), bf16[384,144]{1,0:T(8,128)(2,1)}) %reduce-scatter.31.cloned.1.call-update) | async-done | bytes 110608
  (213 shorter events, 43.9 us)
Async XLA Ops:
  7.2 9.8 %copy-start = (bf16[16,32,768]{2,1,0:T(8,128)(2,1)S(1)}, bf16[16,32,768]{2,1,0:T(8,128)(2,1)}, u32[]{:S(2)}) copy-start(bf16[16,32,768]{2,1,0:T(8,128)(2,1)} %param.15) | copy-start | bytes 2359300
  7.2 99.3 %all-gather.6.cloned.1.call-start = ((), (), s32[]{:S(2)}) async-start(), calls=%async_computation.12 | async-start | bytes 3760128 | tf_op jit(solution)/shard_map/all_gather | solution.py:115
  19.3 12.9 %copy-start.33 = (u32[32]{0:T(128)S(1)}, u32[32]{0:T(128)}, u32[]{:S(2)}) copy-start(u32[32]{0:T(128)} %constant.96) | copy-start | bytes 388
  19.3 14.8 %copy-start.36 = (f32[48]{0:T(128)S(1)}, f32[48]{0:T(128)}, u32[]{:S(2)}) copy-start(f32[48]{0:T(128)} %param.23) | copy-start | bytes 580
  19.3 14.8 %copy-start.37 = (f32[48]{0:T(128)S(1)}, f32[48]{0:T(128)}, u32[]{:S(2)}) copy-start(f32[48]{0:T(128)} %param.24) | copy-start | bytes 580
  19.3 14.8 %copy-start.38 = (f32[48]{0:T(128)S(1)}, f32[48]{0:T(128)}, u32[]{:S(2)}) copy-start(f32[48]{0:T(128)} %param.25) | copy-start | bytes 580
  19.4 14.8 %copy-start.39 = (f32[48]{0:T(128)S(1)}, f32[48]{0:T(128)}, u32[]{:S(2)}) copy-start(f32[48]{0:T(128)} %param.26) | copy-start | bytes 580
  19.4 14.8 %copy-start.40 = (f32[48]{0:T(128)S(1)}, f32[48]{0:T(128)}, u32[]{:S(2)}) copy-start(f32[48]{0:T(128)} %param.27) | copy-start | bytes 580
  19.4 14.8 %copy-start.35 = (f32[192]{0:T(256)S(1)}, f32[192]{0:T(256)}, u32[]{:S(2)}) copy-start(f32[192]{0:T(256)} %param.28) | copy-start | bytes 2308
  25.9 79.1 %all-to-all-start = ((bf16[16,2,12288]{2,1,0:T(2,128)(2,1)}), bf16[16,2,12288]{2,1,0:T(2,128)(2,1)S(1)}, u32[]{:S(2)}, u32[]{:S(2)}) async-start(bf16[16,2,12288]{2,1,0:T(2,128)(2,1)} %reshape.514), calls=%async_computation | async-start | bytes 1572864 | tf_op jit(solution)/shard_map/all_to_all | solution.py:167
  32.2 129.4 %all-gather.8.cloned.1.call-start = ((), (), s32[]{:S(2)}) async-start(), calls=%async_computation.13 | async-start | bytes 4718592 | tf_op jit(solution)/shard_map/all_gather | solution.py:196
  106.1 4.6 copy-start.25
  106.4 4.3 copy-start.29
  106.5 4.2 copy-start.27
  112.2 6.6 copy-start.20
  112.2 16.9 %copy-start.21 = (f32[1536,48]{0,1:T(8,128)S(1)}, f32[1536,48]{0,1:T(8,128)}, u32[]{:S(2)}) copy-start(f32[1536,48]{0,1:T(8,128)} %param.22) | copy-start | bytes 884740
  113.5 25.0 %copy-start.2 = (s32[16]{0:T(128)S(1)}, s32[16]{0:T(128)}, u32[]{:S(2)}) copy-start(s32[16]{0:T(128)} %param.17) | copy-start | bytes 196
  113.5 93.0 %all-gather.10.cloned.1.call-start = ((), (), s32[]{:S(2)}) async-start(), calls=%async_computation.14 | async-start | bytes 1253376 | tf_op jit(solution)/shard_map/all_gather | solution.py:116
  118.7 136.3 %all-gather.12.cloned.1.call-start = ((), (), s32[]{:S(2)}) async-start(), calls=%async_computation.15 | async-start | bytes 5013504 | tf_op jit(solution)/shard_map/all_gather | solution.py:117
  118.8 22.0 %slice-start = ((bf16[1,512,2304]{2,1,0:T(8,128)(2,1)}), bf16[1,512,768]{2,1,0:T(8,128)(2,1)S(1)}, s32[]{:S(2)}) async-start(bf16[1,512,2304]{2,1,0:T(8,128)(2,1)} %copy-done.16), calls=%async_computation.27 | async-start | bytes 1572864 | tf_op jit(solution)/shard_map/slice | solution.py:194
  129.1 179.8 %all-gather.14.cloned.1.call-start = ((), (), s32[]{:S(2)}) async-start(), calls=%async_computation.16 | async-start | bytes 5013504 | tf_op jit(solution)/shard_map/all_gather | solution.py:118
  138.4 252.5 %reduce-scatter.23.cloned.1.call-start = ((), (), s32[]{:S(2)}) async-start(), calls=%async_computation.20 | async-start | bytes 1253376 | tf_op jit(solution)/shard_map/reduce_scatter | solution.py:291
  167.0 15.3 %copy-start.5 = (bf16[1,1024,768]{1,2,0:T(8,128)(2,1)}, bf16[1,1024,768]{1,2,0:T(8,128)(2,1)S(1)}, u32[]{:S(2)}) copy-start(bf16[1,1024,768]{1,2,0:T(8,128)(2,1)S(1)} %copy.50) | copy-start | bytes 4718596
  170.2 24.6 %copy-start.8 = (bf16[1,1024,768]{1,2,0:T(8,128)(2,1)S(1)}, bf16[1,1024,768]{1,2,0:T(8,128)(2,1)}, u32[]{:S(2)}) copy-start(bf16[1,1024,768]{1,2,0:T(8,128)(2,1)} %copy.48) | copy-start | bytes 4718596
  182.3 15.7 %copy-start.3 = (f32[12,512,1024]{2,1,0:T(8,128)S(1)}, f32[12,512,1024]{2,1,0:T(8,128)}, u32[]{:S(2)}) copy-start(f32[12,512,1024]{2,1,0:T(8,128)} %get-tuple-element.103) | copy-start | bytes 75497472
  208.9 114.7 %copy-start.10 = (f32[1,512,768]{2,1,0:T(8,128)}, f32[1,512,768]{2,1,0:T(8,128)S(1)}, u32[]{:S(2)}) copy-start(f32[1,512,768]{2,1,0:T(8,128)S(1)} %get-tuple-element.105) | copy-start | bytes 4718596
  308.8 11.9 %copy-start.34 = (bf16[768,3072]{0,1:T(8,128)(2,1)S(1)}, bf16[768,3072]{0,1:T(8,128)(2,1)}, u32[]{:S(2)}) copy-start(bf16[768,3072]{0,1:T(8,128)(2,1)} %all-gather.12.cloned.1.call-done) | copy-start | bytes 14155780
  320.7 2.9 copy-start.44
  333.9 85.0 %reduce-scatter.19.cloned.1.call-start = ((), (), s32[]{:S(2)}) async-start(), calls=%async_computation.18 | async-start | bytes 2359296 | tf_op jit(solution)/shard_map/reduce_scatter | solution.py:262
  365.0 81.7 %reduce-scatter.17.cloned.1.call-start = ((), (), s32[]{:S(2)}) async-start(), calls=%async_computation.17 | async-start | bytes 2359296 | tf_op jit(solution)/shard_map/reduce_scatter | solution.py:259
  365.0 17.1 %copy-start.7 = (bf16[1,512,768]{1,2,0:T(8,128)(2,1)S(1)}, bf16[1,512,768]{1,2,0:T(8,128)(2,1)}, u32[]{:S(2)}) copy-start(bf16[1,512,768]{1,2,0:T(8,128)(2,1)} %copy.49) | copy-start | bytes 2359300
  382.2 5.3 copy-start.4
  382.2 10.6 %copy-start.11 = (f32[1,512,768]{2,1,0:T(8,128)S(1)}, f32[1,512,768]{2,1,0:T(8,128)}, u32[]{:S(2)}) copy-start(f32[1,512,768]{2,1,0:T(8,128)} %copy-done.10) | copy-start | bytes 4718596
  387.5 73.1 %reduce-scatter.33.cloned.1.call-start = ((), (), s32[]{:S(2)}) async-start(), calls=%async_computation.25 | async-start | bytes 294912
  392.6 147.3 %reduce-scatter.25.cloned.1.call-start = ((), (), s32[]{:S(2)}) async-start(), calls=%async_computation.21 | async-start | bytes 5013504 | tf_op jit(solution)/shard_map/reduce_scatter | solution.py:294
  399.7 219.3 %reduce-scatter.27.cloned.1.call-start = ((), (), s32[]{:S(2)}) async-start(), calls=%async_computation.22 | async-start | bytes 5013504 | tf_op jit(solution)/shard_map/reduce_scatter | solution.py:297
  409.0 37.7 %copy-start.24 = (f32[768]{0:T(1024)S(1)}, f32[768]{0:T(1024)}, u32[]{:S(2)}) copy-start(f32[768]{0:T(1024)} %copy-done.23) | copy-start | bytes 9220
  409.0 37.7 %copy-start.26 = (f32[512]{0:T(512)S(1)}, f32[512]{0:T(512)}, u32[]{:S(2)}) copy-start(f32[512]{0:T(512)} %copy-done.25) | copy-start | bytes 6148
  409.0 37.7 %copy-start.28 = (f32[512]{0:T(512)S(1)}, f32[512]{0:T(512)}, u32[]{:S(2)}) copy-start(f32[512]{0:T(512)} %copy-done.27) | copy-start | bytes 6148
  409.0 37.7 %copy-start.32 = (f32[768]{0:T(1024)S(1)}, f32[768]{0:T(1024)}, u32[]{:S(2)}) copy-start(f32[768]{0:T(1024)} %copy-done.31) | copy-start | bytes 9220
  409.0 281.6 %reduce-scatter.21.cloned.1.call-start = ((), (), s32[]{:S(2)}) async-start(), calls=%async_computation.19 | async-start | bytes 3760128 | tf_op jit(solution)/shard_map/reduce_scatter | solution.py:288
  452.1 252.8 %reduce-scatter.35.cloned.1.call-start = ((), (), s32[]{:S(2)}) async-start(), calls=%async_computation.26 | async-start | bytes 589824
  462.2 4.8 copy-start.30
  610.2 9.1 %copy-start.12 = (f32[1,512,768]{2,1,0:T(8,128)S(1)}, f32[1,512,768]{2,1,0:T(8,128)}, u32[]{:S(2)}) copy-start(f32[1,512,768]{2,1,0:T(8,128)} %copy-done.10) | copy-start | bytes 4718596
  611.3 87.0 %all-to-all-start.1 = ((bf16[16,2,12288]{2,1,0:T(2,128)(2,1)}), bf16[16,2,12288]{2,1,0:T(2,128)(2,1)S(1)}, u32[]{:S(2)}, u32[]{:S(2)}) async-start(bf16[16,2,12288]{2,1,0:T(2,128)(2,1)} %reshape.516), calls=%async_computation.3 | async-start | bytes 1572864 | tf_op jit(solution)/shard_map/all_to_all | solution.py:273
  614.9 104.2 %reduce-scatter.29.cloned.1.call-start = ((), (), s32[]{:S(2)}) async-start(), calls=%async_computation.23 | async-start | bytes 442368 | tf_op jit(solution)/shard_map/reduce_scatter | solution.py:332
  619.0 115.4 %reduce-scatter.31.cloned.1.call-start = ((), (), s32[]{:S(2)}) async-start(), calls=%async_computation.24 | async-start | bytes 589824
  699.0 37.2 %copy-start.1 = (bf16[16,32,768]{2,1,0:T(8,128)(2,1)S(1)}, bf16[16,32,768]{2,1,0:T(8,128)(2,1)}, u32[]{:S(2)}) copy-start(bf16[16,32,768]{2,1,0:T(8,128)(2,1)} %param.15) | copy-start | bytes 2359300
  (15 other events, 25.7 us)
Sparse Core Ops, SparseCore 0:
  15.2 55.1 all-gather.5
  113.6 47.8 all-gather.7
  163.8 36.9 all-gather.9
  203.0 51.9 all-gather.11
  257.1 51.6 all-gather.13
  334.0 56.7 reduce-scatter.22
  393.1 25.1 reduce-scatter.18
  420.5 26.1 reduce-scatter.16
  449.5 11.0 reduce-scatter.32
  464.3 75.5 reduce-scatter.24
  543.7 75.2 reduce-scatter.26
  622.8 67.7 reduce-scatter.20
  692.8 12.0 reduce-scatter.34
  707.0 12.1 reduce-scatter.28
  721.2 13.1 reduce-scatter.30
where the time goes:
time: 751 us; the launch traced here: 743 us
  waiting for transfers between devices  319 us (42%)
  blocking collectives  166 us (22%)
  matrix products  132 us (18%)
  other arithmetic  53.6 us (7%)
  local copies, waits for them, and re-layouts  44 us (6%)
  between operations  17.6 us (2%)
  starting transfers between devices  11.2 us (1%)
    unnamed x2, blocking collectives  129 us
    reduce_scatter x1, waiting for transfers between devices, local(): lax.psum_scatter(grad_up.astype(jnp.bfloat16), 'dp', scatter_dimension=1,...  72 us
    reduce_scatter x1, waiting for transfers between devices, local(): lax.psum_scatter(grad_qkv.astype(jnp.bfloat16), 'dp', scatter_dimension=1...  62.2 us
    all_gather x1, waiting for transfers between devices, fetch_weights(): lax.all_gather(down_part, 'dp', axis=1, tiled=True)  46.8 us
    all_gather x1, waiting for transfers between devices, fetch_weights(): lax.all_gather(up_part, 'dp', axis=1, tiled=True)  45.8 us
    reduce_scatter x1, waiting for transfers between devices, local(): lax.psum_scatter(joined(grad_keys).astype(jnp.bfloat16), 'cp', scatter_di...  27.8 us
    unnamed x117, local copies, waits for them, and re-layouts  24.7 us
    unnamed x18, waiting for transfers between devices  24.5 us
  transfers between devices with their start and end apart: 17, of which 12 were waited for; matrix products, arithmetic and copies ran while one was open for 25% of the time, Pallas kernels for 0%

commit v1 on v0

--- a/solution.py
+++ b/solution.py
@@ -1,9 +1,14 @@
+import functools
 import math
 
 import jax
 import jax.numpy as jnp
 from jax import lax
+from jax.experimental import pallas as pl
+from jax.experimental.pallas import tpu as pltpu
 from jax.sharding import PartitionSpec as P
+
+MESH = pl.DeviceIdType.MESH
 
 HEADS = 12
 HEAD_DIM = 64
@@ -370,6 +375,1136 @@
     )
 
 
+BF16 = jnp.bfloat16
+F32 = jnp.float32
+ROWS = 512
+QUARTER = 256
+WIDE = 768
+HIDDEN = 3072
+PIECE = 32
+SHARDS = ((144, 384), (48, 384), (192, 384), (48, 1536))
+QKV, PROJ, UP, DOWN = range(4)
+G1, C1, BP, G2, C2, BD, BU = range(7)
+
+
+def fits_block(mesh):
+    return mesh.shape["dp"] == 16 and mesh.shape["cp"] == 2
+
+
+def dot_nt(left, right):
+    return lax.dot_general(left, right, (((1,), (1,)), ((), ())), preferred_element_type=F32)
+
+
+def dot_nn(left, right):
+    return lax.dot_general(left, right, (((1,), (0,)), ((), ())), preferred_element_type=F32)
+
+
+def dot_tn(left, right):
+    return lax.dot_general(left, right, (((0,), (0,)), ((), ())), preferred_element_type=F32)
+
+
+def block_kernel(
+    length_ref,
+    xg,
+    cot,
+    wq_in,
+    wp_in,
+    wu_in,
+    wd_in,
+    vec_in,
+    out_ref,
+    ret_ref,
+    gq_out,
+    gp_out,
+    gu_out,
+    gd_out,
+    gvec_out,
+    wq,
+    wp,
+    wu,
+    wd,
+    gq,
+    r0_refs,
+    r1_refs,
+    r2_refs,
+    r3_refs,
+    acts,
+    sems,
+):
+    X, A1, M, KVP, O, R, A2, HD, DU, T1, DRR, G, GT, DKVP, RK, LSE, VEC, VF, CS, VGS, VGR = acts
+    (
+        x_s,
+        x_r,
+        v_s,
+        v_r,
+        c_s,
+        c_r,
+        zs,
+        n1s,
+        n2s,
+        ps,
+        rsem,
+        prsem,
+        kv_s,
+        kv_r,
+        o_s,
+        o_r,
+        r0s,
+        r0r,
+        r1s,
+        r1r,
+        r2s,
+        r2r,
+        r3s,
+        r3r,
+        dk_s,
+        dk_r,
+        ret_s,
+        ret_r,
+        vg_s,
+        vg_r,
+    ) = sems
+    w_refs = (wq, wp, wu, wd)
+    w_in = (wq_in, wp_in, wu_in, wd_in)
+    grads = (gq, wp, wu, wd)
+    g_out = (gq_out, gp_out, gu_out, gd_out)
+
+    dp = lax.axis_index("dp")
+    x = lax.axis_index("cp")
+    z = lax.div(dp, 4)
+    y = lax.rem(lax.div(dp, 2), 2)
+    c = lax.rem(dp, 2)
+    slot = z * 4 + y * 2 + x
+    x1, y1 = x + (1 - c) * (1 - 2 * x), y + c * (1 - 2 * y)
+    x2, y2 = x + c * (1 - 2 * x), y + (1 - c) * (1 - 2 * y)
+
+    def dev(zt, yt, ct, xt):
+        return (zt * 4 + yt * 2 + ct, xt)
+
+    partner = dev(z, y, 1 - c, x)
+    near_one = dev(z, y1, c, x1)
+    near_two = dev(z, y2, c, x2)
+
+    def remote(src, dst, send, recv, target):
+        return pltpu.make_async_remote_copy(
+            src_ref=src,
+            dst_ref=dst,
+            send_sem=send,
+            recv_sem=recv,
+            device_id=target,
+            device_id_type=MESH,
+        )
+
+    def loop(count, body, start=0):
+        def step(k, carry):
+            body(k)
+            return carry
+
+        lax.fori_loop(start, count, step, 0)
+
+    def rows_at(at, count, multiple):
+        return pl.ds(pl.multiple_of(at, multiple), count)
+
+    barrier = pltpu.get_barrier_semaphore()
+    me = dp * 2 + x
+
+    def greet(k):
+        other = lax.rem(me + k, 32)
+        pl.semaphore_signal(
+            barrier,
+            inc=1,
+            device_id=(lax.div(other, 2), lax.rem(other, 2)),
+            device_id_type=MESH,
+        )
+
+    loop(32, greet, 1)
+    pl.semaphore_wait(barrier, 31)
+
+    piece = lax.rem(dp, 8)
+    x_core = lax.rem(x + lax.div(z, 2), 2)
+    x_rows = X.at[rows_at(x * QUARTER + piece * PIECE, PIECE, PIECE), :]
+    x_mine = x_core == c
+
+    def x_copy(k):
+        to = lax.rem(slot + k, 16)
+        target = dev(lax.div(to, 4), lax.rem(lax.div(to, 2), 2), x_core, lax.rem(to, 2))
+        return remote(xg.at[to], x_rows, x_s.at[k], x_r.at[x * 8 + piece], target)
+
+    def x_local():
+        return pltpu.make_async_copy(xg.at[slot], x_rows, x_r.at[x * 8 + piece])
+
+    @pl.when(x_mine)
+    def _():
+        x_local().start()
+
+    @pl.when(jnp.logical_not(x_mine))
+    def _():
+        x_copy(0).start()
+
+    loop(16, lambda k: x_copy(k).start(), 1)
+
+    def v_copy(k):
+        to = lax.rem(dp + k, 16)
+        return remote(vec_in, VEC.at[dp], v_s.at[k], v_r.at[dp], (to, x))
+
+    loop(16, lambda k: v_copy(k).start(), 1)
+    VEC[pl.ds(dp, 1)] = vec_in[...][None]
+
+    def ident(zt, yt, xt):
+        return zt * 4 + yt * 2 + xt
+
+    def shard(ref, m, zt, yt, ct, xt):
+        n, lanes = SHARDS[m]
+        return ref.at[
+            rows_at((zt * 4 + yt * 2 + ct) * n, n, 16), rows_at(xt * lanes, lanes, 128)
+        ]
+
+    def put_own(m):
+        n, lanes = SHARDS[m]
+        w_refs[m][rows_at(dp * n, n, 16), rows_at(x * lanes, lanes, 128)] = w_in[m][...]
+
+    def z_copy(m, k):
+        target = dev(lax.rem(z + k, 4), y, c, x)
+        return remote(
+            w_in[m],
+            shard(w_refs[m], m, z, y, c, x),
+            zs.at[m, k],
+            rsem.at[m, ident(z, y, x)],
+            target,
+        )
+
+    def pass_on(m, first, zt, yt, xt, send, recv, target):
+        place = shard(w_refs[m], m, zt, yt, c, xt)
+        return remote(w_in[m] if first else place, place, send, recv, target)
+
+    def arrived(m, zt, yt, xt):
+        place = shard(w_refs[m], m, zt, yt, c, xt)
+        remote(place, place, zs.at[m, 0], rsem.at[m, ident(zt, yt, xt)], partner).wait_recv()
+
+    def send_one(m, first, k):
+        zt = lax.rem(z + k, 4)
+        return pass_on(
+            m, first, zt, y, x, n1s.at[m, k], rsem.at[m, ident(zt, y, x)], near_one
+        )
+
+    def send_two(m, first, k):
+        zt, yt, xt = (lax.rem(z + k, 4), y, x)
+        return pass_on(
+            m, first, zt, yt, xt, n2s.at[m, k], rsem.at[m, ident(zt, yt, xt)], near_two
+        )
+
+    def send_two_late(m, k):
+        zt = lax.rem(z + k, 4)
+        return pass_on(
+            m, False, zt, y1, x1, n2s.at[m, 4 + k], rsem.at[m, ident(zt, y1, x1)], near_two
+        )
+
+    def far_place(k):
+        late = lax.div(k, 4)
+        zt = lax.rem(z + lax.rem(k, 4), 4)
+        yt = y2 + late * c * (1 - 2 * y2)
+        xt = x2 + late * (1 - c) * (1 - 2 * x2)
+        return zt, yt, xt
+
+    def send_partner(m, first, k, place):
+        zt, yt, xt = place
+        return pass_on(m, first, zt, yt, xt, ps.at[m, k], prsem.at[m, ident(zt, yt, xt)], partner)
+
+    def spread_z(m):
+        loop(4, lambda k: z_copy(m, k).start(), 1)
+
+    def stage_own(m):
+        send_one(m, True, 0).start()
+        send_two(m, True, 0).start()
+        send_partner(m, True, 0, (z, y, x)).start()
+        put_own(m)
+
+    def stage_one(m):
+        def body(k):
+            zt = lax.rem(z + k, 4)
+            arrived(m, zt, y, x)
+            send_one(m, False, k).start()
+            send_two(m, False, k).start()
+            send_partner(m, False, k, (zt, y, x)).start()
+
+        loop(4, body, 1)
+
+    def stage_two(m):
+        def body(k):
+            zt = lax.rem(z + k, 4)
+            arrived(m, zt, y1, x1)
+            send_two_late(m, k).start()
+            send_partner(m, False, 4 + k, (zt, y1, x1)).start()
+
+        loop(4, body)
+
+    def stage_three(m):
+        def body(k):
+            place = far_place(k)
+            arrived(m, *place)
+            send_partner(m, False, 8 + k, place).start()
+
+        loop(8, body)
+
+    def stage_last(m):
+        def body(k):
+            zt, yt, xt = lax.div(k, 4), lax.rem(lax.div(k, 2), 2), lax.rem(k, 2)
+            place = shard(w_refs[m], m, zt, yt, 1 - c, xt)
+            remote(place, place, zs.at[m, 0], prsem.at[m, k], partner).wait_recv()
+
+        loop(16, body)
+
+    def drain_weights(m):
+        loop(4, lambda k: z_copy(m, k).wait_send(), 1)
+        send_one(m, True, 0).wait_send()
+        send_two(m, True, 0).wait_send()
+        send_partner(m, True, 0, (z, y, x)).wait_send()
+
+        def body(k):
+            send_one(m, False, k).wait_send()
+            send_two(m, False, k).wait_send()
+            send_partner(m, False, k, (lax.rem(z + k, 4), y, x)).wait_send()
+
+        loop(4, body, 1)
+
+        def late(k):
+            send_two_late(m, k).wait_send()
+            send_partner(m, False, 4 + k, (lax.rem(z + k, 4), y1, x1)).wait_send()
+
+        loop(4, late)
+        loop(8, lambda k: send_partner(m, False, 8 + k, far_place(k)).wait_send())
+
+    def c_target(h):
+        return lax.rem(x + h, 2)
+
+    def c_copy(h):
+        return remote(
+            cot.at[pl.ds(h * QUARTER, QUARTER), :],
+            G.at[rows_at(x * QUARTER, QUARTER, QUARTER), :],
+            c_s.at[h],
+            c_r.at[x],
+            dev(z, y, c_target(h), c),
+        )
+
+    def c_local(h):
+        return pltpu.make_async_copy(
+            cot.at[pl.ds(h * QUARTER, QUARTER), :],
+            G.at[rows_at(x * QUARTER, QUARTER, QUARTER), :],
+            c_r.at[x],
+        )
+
+    def c_mine(h):
+        return jnp.logical_and(c_target(h) == c, x == c)
+
+    spread_z(QKV)
+    stage_own(QKV)
+    spread_z(PROJ)
+    stage_own(PROJ)
+    spread_z(UP)
+    stage_own(UP)
+    for h in (0, 1):
+
+        @pl.when(c_mine(h))
+        def _(h=h):
+            c_local(h).start()
+
+        @pl.when(jnp.logical_not(c_mine(h)))
+        def _(h=h):
+            c_copy(h).start()
+
+    spread_z(DOWN)
+    stage_own(DOWN)
+
+    stage_one(QKV)
+
+    def v_in(k):
+        to = lax.rem(dp + k, 16)
+        remote(vec_in, VEC.at[to], v_s.at[0], v_r.at[to], (to, x)).wait_recv()
+
+    loop(16, v_in, 1)
+
+    def lane_parts(width, lanes, shift):
+        lane = lax.broadcasted_iota(jnp.int32, (128, lanes), 1).astype(F32)
+        part = jnp.floor((lane + 0.5) * (1.0 / width))
+        row = lax.broadcasted_iota(jnp.int32, (128, lanes), 0).astype(F32)
+        return jnp.where(lane - part * width == row + shift, 1.0, 0.0)
+
+    def lane_owner(width, lanes):
+        lane = lax.broadcasted_iota(jnp.int32, (16, lanes), 1)
+        first = lax.broadcasted_iota(jnp.int32, (16, lanes), 0) * width
+        return jnp.logical_and(lane >= first, lane < first + width)
+
+    pick = lane_parts(48, WIDE, 0.0)
+    owner = lane_owner(48, WIDE)
+    row_in_48 = lax.broadcasted_iota(jnp.int32, (16, 128), 1) < 48
+    for v in range(6):
+        part = jnp.where(row_in_48, VEC[:, v, :], 0.0).astype(BF16)
+        VF[pl.ds(v, 1), pl.ds(0, WIDE)] = jnp.sum(
+            jnp.where(owner, dot_nn(part, pick.astype(BF16)), 0.0), axis=0, keepdims=True
+        )
+
+    def wide_vector(j):
+        at = rows_at(j * WIDE, WIDE, 128)
+        lane = lax.broadcasted_iota(jnp.int32, (128, WIDE), 1).astype(F32)
+        lane = lane - 192.0 * jnp.floor((lane + 0.5) * (1.0 / 192.0))
+        row = lax.broadcasted_iota(jnp.int32, (128, WIDE), 0).astype(F32)
+        low_part = jnp.where(lane == row, 1.0, 0.0)
+        high_part = jnp.where(lane == row + 128.0, 1.0, 0.0)
+        first = lax.broadcasted_iota(jnp.int32, (16, WIDE), 0) * 192 - j * WIDE
+        place = lax.broadcasted_iota(jnp.int32, (16, WIDE), 1)
+        held = jnp.logical_and(place >= first, place < first + 192)
+        return at, low_part, high_part, held
+
+    for j in range(4):
+        at, low_part, high_part, held = wide_vector(j)
+        spread = dot_nn(VEC[:, 6, :].astype(BF16), low_part.astype(BF16)) + dot_nn(
+            VEC[:, 7, :].astype(BF16), high_part.astype(BF16)
+        )
+        VF[pl.ds(BU, 1), at] = jnp.sum(jnp.where(held, spread, 0.0), axis=0, keepdims=True)
+
+    def vector(v, at=0, lanes=WIDE):
+        return VF[pl.ds(v, 1), pl.ds(at, lanes)]
+
+    def x_in(k):
+        place = X.at[rows_at(k * PIECE, PIECE, PIECE), :]
+        remote(place, place, x_s.at[0], x_r.at[k], partner).wait_recv()
+
+    loop(16, x_in)
+
+    def norm_parts(values):
+        centered = values - jnp.mean(values, axis=-1, keepdims=True)
+        spread = jnp.mean(centered * centered, axis=-1, keepdims=True)
+        scale = lax.rsqrt(spread + EPSILON)
+        return centered * scale, scale
+
+    TILE = 128
+
+    def norm_one(i):
+        at = rows_at(i * TILE, TILE, TILE)
+        normal, _ = norm_parts(X[at, :].astype(F32))
+        A1[at, :] = (normal * vector(G1) + vector(C1)).astype(BF16)
+
+    loop(ROWS // TILE, norm_one)
+
+    stage_two(QKV)
+    stage_one(PROJ)
+    stage_three(QKV)
+    stage_last(QKV)
+
+    def mixed(j):
+        at = rows_at(j * QUARTER, QUARTER, QUARTER)
+        M[:, at] = dot_nt(A1[...], wq[at, :]).astype(BF16)
+
+    loop(9, mixed, 3)
+    kv_copy = remote(M.at[:, pl.ds(WIDE, 2 * WIDE)], KVP, kv_s, kv_r, partner)
+    kv_copy.start()
+    stage_two(PROJ)
+    stage_one(UP)
+    loop(3, mixed)
+    stage_three(PROJ)
+    kv_copy.wait_recv()
+
+    lane_half = lax.broadcasted_iota(jnp.int32, (1, 128), 1) < 64
+    offset = lax.broadcasted_iota(jnp.int32, (QUARTER, QUARTER), 1) - lax.broadcasted_iota(
+        jnp.int32, (QUARTER, QUARTER), 0
+    )
+    own_pos = (c * QUARTER, (3 - c) * QUARTER)
+    far_pos = ((1 - c) * QUARTER, (2 + c) * QUARTER)
+
+    def head_lanes(values, e):
+        keep = lane_half if e == 0 else jnp.logical_not(lane_half)
+        return jnp.where(keep, values, jnp.zeros_like(values))
+
+    def masked(scores, key_pos, query_pos):
+        return jnp.where(offset >= key_pos - query_pos, scores, NEG_BIG)
+
+    def scores_of(keys, queries, places, qpos):
+        return [
+            masked(dot_nt(keys[i * QUARTER : (i + 1) * QUARTER], queries), places[i], qpos)
+            for i in range(keys.shape[0] // QUARTER)
+        ]
+
+    def pair_refs(h):
+        at = [rows_at(part * WIDE + h * 128, 128, 128) for part in range(3)]
+        return (
+            M[:, at[0]],
+            M[:, at[1]],
+            M[:, at[2]],
+            KVP[:, at[0]],
+            KVP[:, at[1]],
+        )
+
+    def attend_pair(h):
+        q2, k_own, v_own, k_far, v_far = pair_refs(h)
+        vt_own, vt_far = v_own.T, v_far.T
+        pieces = [[None, None], [None, None]]
+        for e in (0, 1):
+            qm = head_lanes(q2, e) * jnp.asarray(0.125, BF16)
+            for b in (0, 1):
+                span = QUARTER * (b + 1)
+                qs = qm[b * QUARTER : (b + 1) * QUARTER]
+                blocks = scores_of(k_own[:span], qs, own_pos, own_pos[b]) + scores_of(
+                    k_far[:span], qs, far_pos, own_pos[b]
+                )
+                top = functools.reduce(
+                    jnp.maximum, [jnp.max(s, axis=0, keepdims=True) for s in blocks]
+                )
+                exps = [jnp.exp(s - top) for s in blocks]
+                total = functools.reduce(
+                    jnp.add, [jnp.sum(p, axis=0, keepdims=True) for p in exps]
+                )
+                half = len(exps) // 2
+                low_exps = [p.astype(BF16) for p in exps]
+                own_w = jnp.concatenate(low_exps[:half], axis=0) if half > 1 else low_exps[0]
+                far_w = jnp.concatenate(low_exps[half:], axis=0) if half > 1 else low_exps[1]
+                sel = slice(e * 64, (e + 1) * 64)
+                mixed_t = dot_nn(vt_own[sel, :span], own_w) + dot_nn(vt_far[sel, :span], far_w)
+                pieces[b][e] = mixed_t / total
+                LSE[h * 4 + e * 2 + b] = top + jnp.log(total)
+        at = rows_at(h * 128, 128, 128)
+        for b in (0, 1):
+            O[pl.ds(b * QUARTER, QUARTER), at] = (
+                jnp.concatenate(pieces[b], axis=0).T.astype(BF16)
+            )
+
+    fwd_ticks = [
+        lambda: stage_two(UP),
+        lambda: stage_one(DOWN),
+        lambda: stage_three(UP),
+        lambda: stage_two(DOWN),
+    ]
+
+    def attend_step(h):
+        attend_pair(h)
+        for i, tick in enumerate(fwd_ticks):
+            pl.when(h == i + 1)(tick)
+
+    loop(6, attend_step)
+
+    stage_last(PROJ)
+
+    def project(j):
+        at = rows_at(j * QUARTER, QUARTER, QUARTER)
+        R[:, at] = (
+            X[:, at].astype(F32) + dot_nt(O[...], wp[at, :]) + VF[pl.ds(BP, 1), at]
+        )
+
+    loop(3, project)
+
+    def norm_two(i):
+        at = rows_at(i * TILE, TILE, TILE)
+        normal, _ = norm_parts(R[at, :])
+        A2[at, :] = (normal * vector(G2) + vector(C2)).astype(BF16)
+
+    loop(ROWS // TILE, norm_two)
+    stage_last(UP)
+
+    def feed_up(j):
+        at = rows_at(j * QUARTER, QUARTER, QUARTER)
+        u = dot_nt(A2[...], wu[at, :]) + VF[pl.ds(BU, 1), at]
+        square = u * u
+        bent = jnp.tanh(TANH_SCALE * (u + CUBIC_TERM * square * u))
+        half = 0.5 * (1.0 + bent)
+        HD[:, at] = (u * half).astype(BF16)
+        slope = half + 0.5 * u * (1.0 - bent * bent) * (
+            TANH_SCALE + (3.0 * CUBIC_TERM * TANH_SCALE) * square
+        )
+        DU[:, at] = slope.astype(BF16)
+
+    loop(12, feed_up)
+    stage_three(DOWN)
+    stage_last(DOWN)
+
+    length = length_ref[0]
+
+    def live(at_row, count):
+        block = lax.div(at_row, QUARTER)
+        base = own_pos[0] + block * (own_pos[1] - own_pos[0]) + lax.rem(at_row, QUARTER)
+        return lax.broadcasted_iota(jnp.int32, (count, 1), 0) + base < length
+
+    live_rows = jnp.concatenate([live(0, QUARTER), live(QUARTER, QUARTER)], axis=0)
+
+    def feed_down(j):
+        at = rows_at(j * QUARTER, QUARTER, QUARTER)
+        result = R[:, at] + dot_nt(HD[...], wd[at, :]) + VF[pl.ds(BD, 1), at]
+        DRR[:, at] = jnp.where(live_rows, result, 0.0).astype(BF16)
+
+    loop(3, feed_down)
+
+    def o_copy(b):
+        return remote(
+            DRR.at[pl.ds(b * QUARTER, QUARTER), :],
+            out_ref.at[rows_at((c + b - 2 * b * c) * QUARTER, QUARTER, QUARTER), :],
+            o_s.at[b],
+            o_r.at[c],
+            dev(z, y, x, b),
+        )
+
+    def o_local(b):
+        return pltpu.make_async_copy(
+            DRR.at[pl.ds(b * QUARTER, QUARTER), :],
+            out_ref.at[rows_at((c + b - 2 * b * c) * QUARTER, QUARTER, QUARTER), :],
+            o_s.at[b],
+        )
+
+    def o_mine(b):
+        return jnp.logical_and(x == c, x == b)
+
+    for b in (0, 1):
+
+        @pl.when(o_mine(b))
+        def _(b=b):
+            o_local(b).start()
+
+        @pl.when(jnp.logical_not(o_mine(b)))
+        def _(b=b):
+            o_copy(b).start()
+
+    def r0_copy(m, k):
+        n, lanes = SHARDS[m]
+        return remote(
+            grads[m].at[rows_at((k * 2 + 1 - c) * n, n, 16), :],
+            r0_refs[m].at[k],
+            r0s.at[m, k],
+            r0r.at[m, k],
+            partner,
+        )
+
+    def add_in(m, zt, yt, xt, part):
+        n, lanes = SHARDS[m]
+        at = (rows_at((zt * 4 + yt * 2 + c) * n, n, 16), rows_at(xt * lanes, lanes, 128))
+        grads[m][at] = (grads[m][at].astype(F32) + part.astype(F32)).astype(BF16)
+
+    def r1_other(k):
+        a = lax.rem(k, 2)
+        return lax.div(k, 2), (1 - c) * (1 - y) + c * a, (1 - c) * a + c * (1 - x)
+
+    def r1_kept(k):
+        a = lax.rem(k, 2)
+        return lax.div(k, 2), (1 - c) * y + c * a, (1 - c) * a + c * x
+
+    def r1_copy(m, k):
+        zt, yt, xt = r1_other(k)
+        return remote(
+            shard(grads[m], m, zt, yt, c, xt),
+            r1_refs[m].at[k],
+            r1s.at[m, k],
+            r1r.at[m, k],
+            near_two,
+        )
+
+    def r2_copy(m, k):
+        return remote(
+            shard(grads[m], m, k, y1, c, x1), r2_refs[m].at[k], r2s.at[m, k], r2r.at[m, k], near_one
+        )
+
+    def r3_copy(m, k):
+        zt = lax.rem(z + k, 4)
+        return remote(
+            shard(grads[m], m, zt, y, c, x),
+            r3_refs[m].at[k],
+            r3s.at[m, k],
+            r3r.at[m, k],
+            dev(zt, y, c, x),
+        )
+
+    def reduce_start(m):
+        loop(8, lambda k: r0_copy(m, k).start())
+
+    def reduce_core(m):
+        n, lanes = SHARDS[m]
+
+        def body(k):
+            r0_copy(m, k).wait_recv()
+            at = rows_at((k * 2 + c) * n, n, 16)
+            grads[m][at, :] = (grads[m][at, :].astype(F32) + r0_refs[m][k].astype(F32)).astype(
+                BF16
+            )
+
+        def both(k):
+            body(k)
+
+        loop(8, both)
+        loop(8, lambda k: r1_copy(m, k).start())
+
+    def reduce_two(m):
+        def body(k):
+            r1_copy(m, k).wait_recv()
+            zt, yt, xt = r1_kept(k)
+            add_in(m, zt, yt, xt, r1_refs[m][k])
+
+        loop(8, body)
+        loop(4, lambda k: r2_copy(m, k).start())
+
+    def reduce_one(m):
+        def body(k):
+            r2_copy(m, k).wait_recv()
+            add_in(m, k, y, x, r2_refs[m][k])
+
+        loop(4, body)
+        loop(4, lambda k: r3_copy(m, k).start(), 1)
+
+    def reduce_end(m):
+        n, lanes = SHARDS[m]
+        loop(4, lambda k: r3_copy(m, k).wait_recv(), 1)
+        at = (rows_at(dp * n, n, 16), rows_at(x * lanes, lanes, 128))
+        total = grads[m][at].astype(F32)
+        for k in (1, 2, 3):
+            total = total + r3_refs[m][k].astype(F32)
+        g_out[m][...] = total
+
+    def drain_grads(m):
+        loop(8, lambda k: r0_copy(m, k).wait_send())
+        loop(8, lambda k: r1_copy(m, k).wait_send())
+        loop(4, lambda k: r2_copy(m, k).wait_send())
+        loop(4, lambda k: r3_copy(m, k).wait_send(), 1)
+
+    for b in (0, 1):
+        place = G.at[pl.ds(b * QUARTER, QUARTER), :]
+        remote(place, place, c_s.at[0], c_r.at[b], partner).wait_recv()
+    G[...] = jnp.where(live_rows, G[...], jnp.zeros_like(G))
+    GT[...] = G[...].T
+    CS[...] = jnp.zeros_like(CS)
+    CS[pl.ds(BD, 1), pl.ds(0, WIDE)] = jnp.sum(G[...].astype(F32), axis=0, keepdims=True)
+
+    def down_back(j):
+        at = rows_at(j * QUARTER, QUARTER, QUARTER)
+        d_u = (dot_nn(G[...], wd[:, at]) * DU[:, at].astype(F32)).astype(BF16)
+        DU[:, at] = d_u
+        CS[pl.ds(BU, 1), at] = jnp.sum(d_u.astype(F32), axis=0, keepdims=True)
+
+    loop(12, down_back)
+    drain_weights(DOWN)
+
+    def down_grad(j):
+        at = rows_at(j * QUARTER, QUARTER, QUARTER)
+        wd[:, at] = dot_nn(GT[...], HD[:, at]).astype(BF16)
+
+    loop(12, down_grad)
+    reduce_start(DOWN)
+
+    def up_back(j):
+        at = rows_at(j * QUARTER, QUARTER, QUARTER)
+        T1[:, at] = dot_nn(DU[...], wu[:, at])
+
+    loop(3, up_back)
+    drain_weights(UP)
+    reduce_core(DOWN)
+
+    def up_grad(j):
+        at = rows_at(j * QUARTER, QUARTER, QUARTER)
+        wu[at, :] = dot_tn(DU[:, at], A2[...]).astype(BF16)
+
+    loop(12, up_grad)
+    reduce_start(UP)
+
+    for b in (0, 1):
+
+        @pl.when(o_mine(b))
+        def _(b=b):
+            o_local(b).wait()
+
+        @pl.when(jnp.logical_not(o_mine(b)))
+        def _(b=b):
+            o_copy(b).wait_send()
+
+    def add_rows(v, values):
+        CS[pl.ds(v, 1), pl.ds(0, WIDE)] += jnp.sum(values, axis=0, keepdims=True)
+
+    def norm_two_back(i):
+        at = rows_at(i * TILE, TILE, TILE)
+        normal, scale = norm_parts(R[at, :])
+        d_a = T1[at, :]
+        e = d_a * vector(G2)
+        inner = (
+            e
+            - jnp.mean(e, axis=-1, keepdims=True)
+            - normal * jnp.mean(e * normal, axis=-1, keepdims=True)
+        )
+        d_r = G[at, :].astype(F32) + inner * scale
+        T1[at, :] = d_r
+        DRR[at, :] = d_r.astype(BF16)
+        add_rows(G2, d_a * normal)
+        add_rows(C2, d_a)
+        add_rows(BP, d_r)
+
+    loop(ROWS // TILE, norm_two_back)
+    reduce_core(UP)
+    reduce_two(DOWN)
+
+    def project_back(j):
+        at = rows_at(j * QUARTER, QUARTER, QUARTER)
+        A2[:, at] = dot_nn(DRR[...], wp[:, at]).astype(BF16)
+
+    loop(3, project_back)
+    drain_weights(PROJ)
+
+    def project_grad(j):
+        at = rows_at(j * QUARTER, QUARTER, QUARTER)
+        wp[at, :] = dot_tn(DRR[:, at], O[...]).astype(BF16)
+
+    loop(3, project_grad)
+    reduce_start(PROJ)
+    kv_copy.wait_send()
+
+    def dk_copy(h, part):
+        at = rows_at(part * WIDE + h * 128, 128, 128)
+        return remote(DKVP.at[:, at], RK.at[:, at], dk_s.at[h, part], dk_r.at[h, part], partner)
+
+    def attend_back(h):
+        q2, k_own, v_own, k_far, v_far = pair_refs(h)
+        do2 = A2[:, rows_at(h * 128, 128, 128)]
+        kt_own, kt_far = k_own.T, k_far.T
+        dq = [[None, None], [None, None]]
+        d_keys = [None] * 4
+        d_vals = [None] * 4
+
+        def gather(store, i, value):
+            store[i] = value if store[i] is None else store[i] + value
+
+        for e in (0, 1):
+            qm = head_lanes(q2, e) * jnp.asarray(0.125, BF16)
+            dom = head_lanes(do2, e)
+            for b in (0, 1):
+                span = QUARTER * (b + 1)
+                rows = slice(b * QUARTER, (b + 1) * QUARTER)
+                qs, dos = qm[rows], dom[rows]
+                log_total = LSE[h * 4 + e * 2 + b]
+                blocks = scores_of(k_own[:span], qs, own_pos, own_pos[b]) + scores_of(
+                    k_far[:span], qs, far_pos, own_pos[b]
+                )
+                weights = [jnp.exp(s - log_total) for s in blocks]
+                values = [v_own[i * QUARTER : (i + 1) * QUARTER] for i in range(b + 1)] + [
+                    v_far[i * QUARTER : (i + 1) * QUARTER] for i in range(b + 1)
+                ]
+                d_w = [dot_nt(v, dos) for v in values]
+                delta = functools.reduce(
+                    jnp.add,
+                    [jnp.sum(p * d, axis=0, keepdims=True) for p, d in zip(weights, d_w)],
+                )
+                d_s = [(p * (d - delta)).astype(BF16) for p, d in zip(weights, d_w)]
+                sel = slice(e * 64, (e + 1) * 64)
+                total = None
+                for i, d in enumerate(d_s):
+                    kt = kt_own if i <= b else kt_far
+                    j = i if i <= b else i - b - 1
+                    term = dot_nn(kt[sel, j * QUARTER : (j + 1) * QUARTER], d)
+                    total = term if total is None else total + term
+                    where = j if i <= b else 2 + j
+                    gather(d_keys, where, dot_nn(d, qs))
+                    gather(d_vals, where, dot_nn(weights[i].astype(BF16), dos))
+                dq[b][e] = total * 0.125
+        for b in (0, 1):
+            M[pl.ds(b * QUARTER, QUARTER), rows_at(h * 128, 128, 128)] = (
+                jnp.concatenate(dq[b], axis=0).T.astype(BF16)
+            )
+        for part, store in ((0, d_keys), (1, d_vals)):
+            for i in (0, 1):
+                rows = pl.ds(i * QUARTER, QUARTER)
+                M[rows, rows_at((1 + part) * WIDE + h * 128, 128, 128)] = store[i].astype(BF16)
+                DKVP[rows, rows_at(part * WIDE + h * 128, 128, 128)] = store[2 + i].astype(BF16)
+        for part in (0, 1):
+            dk_copy(h, part).start()
+
+    bwd_ticks = [
+        lambda: reduce_core(PROJ),
+        lambda: reduce_two(UP),
+        lambda: reduce_one(DOWN),
+        lambda: reduce_two(PROJ),
+        lambda: reduce_one(UP),
+    ]
+
+    def attend_back_step(h):
+        attend_back(h)
+        for i, tick in enumerate(bwd_ticks):
+            pl.when(h == i)(tick)
+
+    loop(6, attend_back_step)
+
+    def settle(h):
+        for part in (0, 1):
+            dk_copy(h, part).wait_recv()
+            at = rows_at((1 + part) * WIDE + h * 128, 128, 128)
+            M[:, at] = (
+                M[:, at].astype(F32) + RK[:, rows_at(part * WIDE + h * 128, 128, 128)].astype(F32)
+            ).astype(BF16)
+
+    loop(6, settle)
+
+    def qkv_grad(j):
+        at = rows_at(j * QUARTER, QUARTER, QUARTER)
+        gq[at, :] = dot_tn(M[:, at], A1[...]).astype(BF16)
+
+    loop(9, qkv_grad)
+    reduce_start(QKV)
+    reduce_one(PROJ)
+
+    grad_first = R
+
+    def qkv_back(j):
+        at = rows_at(j * QUARTER, QUARTER, QUARTER)
+        grad_first[:, at] = dot_nn(M[...], wq[:, at])
+
+    loop(3, qkv_back)
+    reduce_core(QKV)
+
+    def norm_one_back(i):
+        at = rows_at(i * TILE, TILE, TILE)
+        normal, scale = norm_parts(X[at, :].astype(F32))
+        d_a = grad_first[at, :]
+        e = d_a * vector(G1)
+        inner = (
+            e
+            - jnp.mean(e, axis=-1, keepdims=True)
+            - normal * jnp.mean(e * normal, axis=-1, keepdims=True)
+        )
+        A2[at, :] = (T1[at, :] + inner * scale).astype(BF16)
+        add_rows(G1, d_a * normal)
+        add_rows(C1, d_a)
+
+    loop(ROWS // TILE, norm_one_back)
+
+    def ret_place(k):
+        b, r = lax.div(k, 8), lax.rem(k, 8)
+        zt = 2 * lax.rem(c + b, 2) + lax.div(r, 4)
+        return zt, lax.rem(lax.div(r, 2), 2), lax.rem(r, 2), b
+
+    def ret_copy(k):
+        return remote(
+            A2.at[rows_at(k * PIECE, PIECE, PIECE), :],
+            ret_ref.at[slot],
+            ret_s.at[k],
+            ret_r.at[slot],
+            dev(*ret_place(k)),
+        )
+
+    def ret_local(k):
+        return pltpu.make_async_copy(
+            A2.at[rows_at(k * PIECE, PIECE, PIECE), :], ret_ref.at[slot], ret_s.at[k]
+        )
+
+    def ret_mine(k):
+        zt, yt, ct, xt = ret_place(k)
+        return (zt * 4 + yt * 2 + ct) * 2 + xt == me
+
+    def ret_start(k):
+        pl.when(ret_mine(k))(lambda: ret_local(k).start())
+        pl.when(jnp.logical_not(ret_mine(k)))(lambda: ret_copy(k).start())
+
+    def ret_end(k):
+        pl.when(ret_mine(k))(lambda: ret_local(k).wait())
+        pl.when(jnp.logical_not(ret_mine(k)))(lambda: ret_copy(k).wait_send())
+
+    loop(16, ret_start)
+
+    highest = lax.Precision.HIGHEST
+    for v in range(6):
+        spread = jnp.where(owner, CS[pl.ds(v, 1), pl.ds(0, WIDE)], 0.0)
+        VGS[:, v, :] = lax.dot_general(
+            spread, pick, (((1,), (1,)), ((), ())), precision=highest, preferred_element_type=F32
+        )
+    lows, highs = (None, None)
+    for j in range(4):
+        at, low_part, high_part, held = wide_vector(j)
+        spread = jnp.where(held, CS[pl.ds(BU, 1), at], 0.0)
+        a = lax.dot_general(
+            spread, low_part, (((1,), (1,)), ((), ())), precision=highest, preferred_element_type=F32
+        )
+        b = lax.dot_general(
+            spread, high_part, (((1,), (1,)), ((), ())), precision=highest, preferred_element_type=F32
+        )
+        lows, highs = (a, b) if lows is None else (lows + a, highs + b)
+    VGS[:, 6, :] = lows
+    VGS[:, 7, :] = highs
+
+    def vg_copy(k):
+        other = lax.rem(me + k, 32)
+        to = lax.div(other, 2)
+        return remote(
+            VGS.at[to], VGR.at[me], vg_s.at[k], vg_r.at[me], (to, lax.rem(other, 2))
+        )
+
+    def vg_in(k):
+        other = lax.rem(me + k, 32)
+        remote(VGS.at[0], VGR.at[other], vg_s.at[0], vg_r.at[other], partner).wait_recv()
+
+    loop(32, lambda k: vg_copy(k).start(), 1)
+    VGR[pl.ds(me, 1)] = VGS[pl.ds(dp, 1)]
+
+    reduce_two(QKV)
+    reduce_one(QKV)
+    for m in (DOWN, UP, PROJ):
+        reduce_end(m)
+    loop(32, vg_in, 1)
+    gvec_out[...] = jnp.sum(VGR[...], axis=0)
+    reduce_end(QKV)
+
+    def ret_in(k):
+        remote(A2.at[pl.ds(0, PIECE), :], ret_ref.at[k], ret_s.at[0], ret_r.at[k], partner).wait_recv()
+
+    def ret_wait(k):
+        stays = jnp.logical_and(k == slot, x_mine)
+        pl.when(jnp.logical_not(stays))(lambda: ret_in(k))
+
+    loop(16, ret_wait)
+
+    def o_in(b):
+        place = out_ref.at[pl.ds(0, QUARTER), :]
+        remote(place, place, o_s.at[0], o_r.at[b], partner).wait_recv()
+
+    for b in (0, 1):
+        stays = jnp.logical_and(x == c, c == b)
+        pl.when(jnp.logical_not(stays))(functools.partial(o_in, b))
+
+    pl.when(x_mine)(lambda: None)
+    pl.when(jnp.logical_not(x_mine))(lambda: x_copy(0).wait_send())
+    loop(16, lambda k: x_copy(k).wait_send(), 1)
+    loop(16, lambda k: v_copy(k).wait_send(), 1)
+    for h in (0, 1):
+        pl.when(jnp.logical_not(c_mine(h)))(functools.partial(lambda h: c_copy(h).wait_send(), h))
+    drain_weights(QKV)
+    for m in range(4):
+        drain_grads(m)
+
+    def dk_end(h):
+        for part in (0, 1):
+            dk_copy(h, part).wait_send()
+
+    loop(6, dk_end)
+    loop(16, ret_end)
+    loop(32, lambda k: vg_copy(k).wait_send(), 1)
+
+
+def block_local(
+    x_source,
+    cotangent,
+    lengths,
+    dealing,
+    qkv_weight,
+    proj_weight,
+    up_weight,
+    down_weight,
+    *vectors,
+):
+    slots = x_source.shape[0]
+    places = jnp.arange(slots, dtype=jnp.int32)
+    owners = jnp.sum(jnp.where(dealing[None, :] == places[:, None], places[None, :], 0), axis=1)
+    dp = lax.axis_index("dp")
+    slot = (dp // 2) * 2 + lax.axis_index("cp")
+    length = jnp.sum(jnp.where(dealing == slot, lengths, 0)).reshape(1)
+    gathered = x_source[owners]
+    first_gain, first_shift, proj_bias, second_gain, second_shift, up_bias, down_bias = vectors
+    narrow = [
+        jnp.pad(vector, (0, 128 - vector.shape[0]))
+        for vector in (first_gain, first_shift, proj_bias, second_gain, second_shift, down_bias)
+    ]
+    up_rows = jnp.pad(up_bias, (0, 256 - up_bias.shape[0])).reshape(2, 128)
+    packed = jnp.concatenate([jnp.stack(narrow), up_rows]).astype(BF16).astype(F32)
+    weights = [
+        weight.astype(BF16).T for weight in (qkv_weight, proj_weight, up_weight, down_weight)
+    ]
+    vmem = pl.BlockSpec(memory_space=pltpu.VMEM)
+    smem = pl.BlockSpec(memory_space=pltpu.SMEM)
+    dma = pltpu.SemaphoreType.DMA
+
+    def act(*shape, dtype=BF16):
+        return pltpu.VMEM(shape, dtype)
+
+    full = [act(16 * n, 2 * lanes) for n, lanes in SHARDS]
+    acts = (
+        act(ROWS, WIDE),
+        act(ROWS, WIDE),
+        act(ROWS, 3 * WIDE),
+        act(ROWS, 2 * WIDE),
+        act(ROWS, WIDE),
+        act(ROWS, WIDE, dtype=F32),
+        act(ROWS, WIDE),
+        act(ROWS, HIDDEN),
+        act(ROWS, HIDDEN),
+        act(ROWS, WIDE, dtype=F32),
+        act(ROWS, WIDE),
+        act(ROWS, WIDE),
+        act(WIDE, ROWS),
+        act(ROWS, 2 * WIDE),
+        act(ROWS, 2 * WIDE),
+        act(24, 1, QUARTER, dtype=F32),
+        act(16, 8, 128, dtype=F32),
+        act(8, HIDDEN, dtype=F32),
+        act(8, HIDDEN, dtype=F32),
+        act(16, 8, 128, dtype=F32),
+        act(32, 8, 128, dtype=F32),
+    )
+    sems = (
+        dma((16,)),
+        dma((16,)),
+        dma((16,)),
+        dma((16,)),
+        dma((2,)),
+        dma((2,)),
+        dma((4, 4)),
+        dma((4, 4)),
+        dma((4, 8)),
+        dma((4, 16)),
+        dma((4, 16)),
+        dma((4, 16)),
+        dma,
+        dma,
+        dma((2,)),
+        dma((2,)),
+        dma((4, 8)),
+        dma((4, 8)),
+        dma((4, 8)),
+        dma((4, 8)),
+        dma((4, 4)),
+        dma((4, 4)),
+        dma((4, 4)),
+        dma((4, 4)),
+        dma((6, 2)),
+        dma((6, 2)),
+        dma((16,)),
+        dma((16,)),
+        dma((32,)),
+        dma((32,)),
+    )
+    results = pl.pallas_call(
+        block_kernel,
+        out_shape=(
+            jax.ShapeDtypeStruct((ROWS, WIDE), BF16),
+            jax.ShapeDtypeStruct((16, PIECE, WIDE), BF16),
+            *[jax.ShapeDtypeStruct(shard, F32) for shard in SHARDS],
+            jax.ShapeDtypeStruct((8, 128), F32),
+        ),
+        in_specs=[smem] + [vmem] * 7,
+        out_specs=(vmem,) * 7,
+        scratch_shapes=[
+            *full,
+            act(16 * SHARDS[QKV][0], 2 * SHARDS[QKV][1]),
+            tuple(act(8, n, 2 * lanes) for n, lanes in SHARDS),
+            tuple(act(8, n, lanes) for n, lanes in SHARDS),
+            tuple(act(4, n, lanes) for n, lanes in SHARDS),
+            tuple(act(4, n, lanes) for n, lanes in SHARDS),
+            acts,
+            sems,
+        ],
+        compiler_params=pltpu.CompilerParams(
+            collective_id=0, has_side_effects=True, vmem_limit_bytes=67043328
+        ),
+        name="block_step",
+    )(length, gathered, cotangent[0], *weights, packed)
+    output, returned, gq, gp, gu, gd, gvec = results
+    owned = [gvec[v, : vector.shape[0]] for v, vector in ((G1, first_gain), (C1, first_shift))]
+    owned += [gvec[v, : proj_bias.shape[0]] for v in (BP, G2, C2)]
+    owned += [gvec[6:8].reshape(-1)[: up_bias.shape[0]], gvec[BD, : down_bias.shape[0]]]
+    return (
+        output[None],
+        returned[dealing],
+        gq.T,
+        gp.T,
+        gu.T,
+        gd.T,
+        *owned,
+    )
+
 def solution(mesh):
     in_specs = (
         P(None, ("cp", "dp"), None),
@@ -403,4 +1538,5 @@
         P("dp"),
         P("dp"),
     )
-    return jax.shard_map(local, mesh=mesh, in_specs=in_specs, out_specs=out_specs, check_vma=False)
+    step = block_local if fits_block(mesh) else local
+    return jax.shard_map(step, mesh=mesh, in_specs=in_specs, out_specs=out_specs, check_vma=False)

time: 751 us -> 255 us (0.34)
  waiting for transfers between devices: 319 us -> 0 us
  Pallas kernels: 0 us -> 228 us
  blocking collectives: 166 us -> 0 us
  matrix products: 132 us -> 0 us
  other arithmetic: 53.6 us -> 4.53 us
  local copies, waits for them, and re-layouts: 44 us -> 18.4 us
  between operations: 17.6 us -> 0.76 us
  starting transfers between devices: 11.2 us -> 0 us
    pallas_call x0 -> x1, Pallas kernels: none -> 228 us  [block_local(): pl.pallas_call(block_kernel, out_shape=(jax.ShapeDtypeStruct((ROWS, WIDE)...]
    reduce_scatter x7 -> x0, waiting for transfers between devices: 182 us -> none  [the longest x1 72 us: local(): lax.psum_scatter(grad_up.astype(jnp.bfloat16), 'dp', scatter_dimension=1,...]
    dot_general x18 -> x0, matrix products: 132 us -> none  [the longest x4 22.8 us: mat_back(): jnp.einsum('sqe,de->sqd', left, right, preferred_element_type=jnp.float32)]
    unnamed x2 -> x0, blocking collectives: 129 us -> none
    all_gather x5 -> x0, waiting for transfers between devices: 112 us -> none  [the longest x1 46.8 us: fetch_weights(): lax.all_gather(down_part, 'dp', axis=1, tiled=True)]
    all_gather x4 -> x0, blocking collectives: 31.3 us -> none  [the longest x1 10.2 us: fetch_weights(): lax.all_gather(up_weight.astype(jnp.bfloat16), 'cp', axis=0, tiled=True)]
    unnamed x18 -> x0, waiting for transfers between devices: 24.5 us -> none
    convert_element_type x27 -> x1, other arithmetic: 22.3 us -> 0.6 us  [block_local(): jnp.concatenate([jnp.stack(narrow), up_rows]).astype(BF16).astype(F32)]
  transfers between devices with their start and end apart: 17 -> 0, of which waited for: 12 -> 0; matrix products, arithmetic and copies ran while one was open for 25% -> 0% of each run, Pallas kernels for 0% -> 0%
where the time goes in v1:
time: 255 us; the launch traced here: 252 us
  Pallas kernels  228 us (89%)
  local copies, waits for them, and re-layouts  18.4 us (7%)
  other arithmetic  4.53 us (2%)
    pallas_call x1, Pallas kernels, block_local(): pl.pallas_call(block_kernel, out_shape=(jax.ShapeDtypeStruct((ROWS, WIDE)...  228 us
    unnamed x45, local copies, waits for them, and re-layouts  11.9 us

profile of v1, /device:TPU:0, one launch (start us, length us, event | category | flops | bytes accessed | tf_op | source)
XLA Modules:
  0.0 252.2 jit_solution(3525900052485374922)
XLA Ops:
  0.7 0.0 copy-start.11
  0.7 0.0 copy-start.12
  0.7 0.6 copy-done.11
  1.3 0.0 copy-done.12
  1.3 1.1 compare_select_fusion
  2.5 0.0 copy-start.14
  2.5 0.7 copy-done.14
  3.1 0.0 copy-start.15
  3.1 0.6 copy-done.15
  3.8 0.0 copy-start.16
  3.8 0.6 copy-done.16
  4.5 0.0 copy-start.17
  4.5 0.6 copy-done.17
  5.1 0.0 copy-start.18
  5.1 0.6 copy-done.18
  5.8 0.0 copy-start.19
  5.8 0.6 copy-done.19
  6.4 0.0 copy-start.13
  6.5 0.7 copy-done.13
  7.2 0.6 convert_element_type.29.vec_in
  7.8 0.1 select_reduce_fusion
  7.9 0.0 copy-start.1
  7.9 2.7 %gather_fusion = bf16[16,32,768]{2,1,0:T(8,128)(2,1)} fusion(bf16[16,32,768]{2,1,0:T(8,128)(2,1)} %param.15, s32[1024]{0:T(1024)S(1)} %pad_clamp_fusion.1), kind=kCustom, calls=%fused_computation | custom fusion | bytes 1572928 | tf_op jit(solution)/shard_map/gather | solution.py:1395
  10.6 0.0 copy-done.1
  10.6 0.7 convert_bitcast_fusion.wd_in
  11.3 0.3 copy-done.2
  11.6 0.7 convert_bitcast_fusion.1.wu_in
  12.3 0.3 copy-done.6
  12.6 0.7 convert_bitcast_fusion.2.wq_in
  13.2 0.2 copy-done.7
  13.5 0.6 convert_bitcast_fusion.3.wp_in
  14.1 228.5 %block_step.1 = (bf16[512,768]{1,0:T(8,128)(2,1)}, bf16[16,32,768]{2,1,0:T(8,128)(2,1)}, f32[144,384]{1,0:T(8,128)}, f32[48,384]{1,0:T(8,128)}, f32[192,384]{1,0...) custom-call(s32[1]{0:T(128)} %bitcast.length_ref, bf16[16,32,768]{2,1,0:T(8,128)(2,1)} %gather_fusion, ...), custom_call_target="tpu_custom_call" | custom-call | tf_op jit(solution)/shard_map/block_step/pallas_call | solution.py:1469
  242.6 0.0 copy-start.10
  242.6 0.6 copy-done.10
  243.2 2.7 %gather_fusion.1 = bf16[16,32,768]{2,1,0:T(8,128)(2,1)} fusion(bf16[16,32,768]{2,1,0:T(8,128)(2,1)} %get-tuple-element.21, s32[1024]{0:T(1024)S(1)} %pad_clamp_fusion), kind=kCustom, calls=%fused_computation.1 | custom fusion | bytes 1572928 | tf_op jit(solution)/shard_map/gather | solution.py:1500
  245.9 0.7 copy-done.9
  246.6 0.5 slice_bitcast_fusion.1
  247.1 0.6 slice_bitcast_fusion
  247.7 0.0 copy-done
  247.7 0.9 copy.33
  248.6 0.3 copy-done.5
  248.9 0.7 copy.34
  249.5 0.2 copy-done.8
  249.8 0.6 copy.35
  250.4 0.0 copy-done.4
  250.4 0.7 copy.36
  251.1 0.4 copy-done.3
  251.5 0.7 copy.37
  (24 shorter events, 0.1 us)
Async XLA Ops:
  0.7 0.7 copy-start.11
  0.7 0.7 copy-start.12
  2.5 0.7 copy-start.14
  3.1 0.7 copy-start.15
  3.8 0.7 copy-start.16
  4.5 0.7 copy-start.17
  5.1 0.7 copy-start.18
  5.8 0.7 copy-start.19
  6.4 0.7 copy-start.13
  7.9 2.7 %copy-start.1 = (f32[1536,48]{0,1:T(8,128)S(1)}, f32[1536,48]{0,1:T(8,128)}, u32[]{:S(2)}) copy-start(f32[1536,48]{0,1:T(8,128)} %param.22) | copy-start | bytes 884740
  10.6 1.0 copy-start.2
  11.6 1.0 copy-start.6
  12.6 0.9 copy-start.7
  242.6 0.7 copy-start.10
  243.2 4.5 %copy-start = (bf16[512,768]{1,0:T(8,128)(2,1)S(1)}, bf16[512,768]{1,0:T(8,128)(2,1)}, u32[]{:S(2)}) copy-start(bf16[512,768]{1,0:T(8,128)(2,1)} %get-tuple-element.20) | copy-start | bytes 2359300
  245.9 0.7 copy-start.9
  247.7 1.1 copy-start.5
  248.9 0.9 copy-start.8
  248.9 1.5 copy-start.4
  250.4 1.1 copy-start.3
